TPU v7x, 128 devices: a whole 4x4x4 slice. The times are simulated.
128 devices in a mesh: rep: 8 (over y, x_hi), tp: 16 (over x_lo, z, core).
Axes of the slice: x: 4 (x_hi: 2, x_lo: 2; x = x_hi * 2 + x_lo), y: 4, z: 4, core: 2. Of those that a mesh axis runs over, the one named last changes fastest.
Arguments:
- hidden: bfloat16 [4096, 14336], P('rep'), may hold values from -6 to 6
- ln_gain: float32 [14336], replicated, may hold values from 0.1 to 1.9
- ln_shift: float32 [14336], replicated, may hold values from -3 to 3
- qkv_weight: bfloat16 [14336, 32, 384], P(('rep', 'tp')), may hold values from -0.046875 to 0.046875
- qkv_bias: float32 [32, 384], P('tp'), may hold values from -64 to 64
- out_weight: bfloat16 [14336, 32, 128], P('tp'), may hold values from -0.375 to 0.375
- out_bias: float32 [14336], P('tp'), may hold values from -3 to 3
- slope_index: int32 [32], P('tp'), may hold values from 0 to 111
Outputs:
- attended: bfloat16 [4096, 14336], P('rep', 'tp')
All inputs are finite; a program needn't handle non-finite values.
Results may differ from a plain program's by a relative error of at most 0.024.
The roundings to bfloat16 on the way count: a program that leaves them out, or rounds other values in their place, can miss the bound.
Values may be sent and summed in bfloat16 or wider, within the bound.
A program may use at most 192 MiB of HBM per device.

v0:
```python
import math

import jax
import jax.numpy as jnp
from jax import lax
from jax.sharding import PartitionSpec as P

N_SLOPES = 112


epsilon = 1e-05


def slope_values(slope_index):
    power = 1 << N_SLOPES.bit_length() - 1
    index_float = slope_index.astype(jnp.float32)
    leading = jnp.exp2(-8.0 * (index_float + 1.0) / power)
    between = jnp.exp2(-4.0 * (2.0 * (index_float - power) + 1.0) / power)
    return jnp.where(slope_index < power, leading, between)


def layer_norm(hidden, ln_gain, ln_shift):
    inputs_f32 = hidden.astype(jnp.float32)
    average = jnp.mean(inputs_f32, axis=-1, keepdims=True)
    centred = inputs_f32 - average
    variance = jnp.mean(centred * centred, axis=-1, keepdims=True)
    return (centred * lax.rsqrt(variance + epsilon) * ln_gain + ln_shift).astype(jnp.bfloat16)


def shards(hidden, ln_gain, ln_shift, qkv_weight, qkv_bias, out_weight, out_bias, slope_index):
    seq_rows = hidden.shape[0]
    heads_here = qkv_bias.shape[0]
    head_size = qkv_bias.shape[1] // 3
    flat_width = heads_here * 3 * head_size
    normed = layer_norm(hidden, ln_gain, ln_shift)
    regrouped = lax.all_to_all(qkv_weight, "tp", split_axis=1, concat_axis=0, tiled=True)
    weight_piece = lax.all_gather(regrouped, "rep", axis=0, tiled=True)
    flat_piece = weight_piece.reshape(weight_piece.shape[0], flat_width)
    projected = jnp.dot(normed, flat_piece, preferred_element_type=jnp.float32)
    qkv = (projected.reshape(seq_rows, heads_here, 3 * head_size) + qkv_bias).astype(jnp.bfloat16)
    query = qkv[:, :, :head_size]
    keys = qkv[:, :, head_size : 2 * head_size]
    values = qkv[:, :, 2 * head_size :]
    slopes = slope_values(slope_index)
    scores = jnp.einsum(
        "sha,tha->hst", query, keys, preferred_element_type=jnp.float32
    ) / math.sqrt(head_size)
    position = lax.iota(jnp.int32, seq_rows)
    distance = (position[:, None] - position[None, :]).astype(jnp.float32)
    scores = scores - slopes[:, None, None] * distance
    scores = jnp.where(distance >= 0.0, scores, -1e30)
    highest = jnp.max(scores, axis=-1, keepdims=True)
    powered = jnp.exp(scores - highest)
    attention = (powered / jnp.sum(powered, axis=-1, keepdims=True)).astype(jnp.bfloat16)
    context = jnp.einsum(
        "hst,tha->sha", attention, values, preferred_element_type=jnp.float32
    ).astype(jnp.bfloat16)
    context = context.reshape(seq_rows, heads_here * head_size)
    everything = lax.all_gather(context, "tp", axis=1, tiled=True)
    groups = lax.axis_size("tp")
    group_width = heads_here * head_size
    context_blocks = everything.reshape(seq_rows, groups, group_width)
    weight_blocks = out_weight.reshape(out_weight.shape[0], groups, group_width)
    partials = jnp.einsum(
        "sgk,dgk->gsd", context_blocks, weight_blocks, preferred_element_type=jnp.float32
    ).astype(jnp.bfloat16)
    partials = lax.optimization_barrier(partials)
    result = jnp.sum(partials.astype(jnp.float32), axis=0) + out_bias
    return result.astype(jnp.bfloat16)


def solution(mesh):
    return jax.shard_map(
        shards,
        mesh=mesh,
        in_specs=(
            P("rep", None),
            P(),
            P(),
            P(("rep", "tp"), None, None),
            P("tp", None),
            P("tp", None, None),
            P("tp"),
            P("tp"),
        ),
        out_specs=P("rep", "tp"),
        check_vma=False,
    )
```

profile of v0, /device:TPU:1, one launch (start us, length us, event | category | flops | bytes accessed | tf_op | source)
XLA Modules:
  0.0 399.7 jit_solution(10070072146498777757)
XLA Ops:
  6.5 0.0 all-gather.3.cloned.1.call-start
  6.5 2.8 copy.16
  9.3 41.7 %all_to_all.18 = bf16[112,32,384]{2,0,1:T(8,128)(2,1)S(1)} all-to-all(bf16[112,32,384]{2,0,1:T(8,128)(2,1)S(1)} %copy.16), channel_id=1, replica_groups=mesh['rep'=8,'tp'=16] {'tp'}, dimensions={1} | all-to-all | bytes 5505024 | tf_op jit(solution)/shard_map/all_to_all | solution.py:36
  51.0 1.8 copy.17
  52.8 0.0 copy-start.5
  52.8 0.0 all-gather.3.cloned.1.call-update
  52.9 0.0 all-gather.5.cloned.1.call-start
  52.9 0.2 broadcast_compare_fusion
  53.1 0.1 subtract_convert_fusion
  53.3 0.2 copy-done.5
  53.5 7.2 %convert_reduce_fusion = f32[512]{0:T(512)S(1)} fusion(bf16[512,14336]{1,0:T(8,128)(2,1)} %param.8), kind=kLoop, calls=%fused_computation.2 | loop fusion | flops 14679552 | bytes 14682112 | tf_op jit(solution)/shard_map/reduce_sum | solution.py:24
  60.7 11.6 %fusion.3 = f32[512]{0:T(512)S(1)} fusion(bf16[512,14336]{1,0:T(8,128)(2,1)} %param.8, f32[512]{0:T(512)S(1)} %broadcast_multiply_fusion), kind=kLoop, calls=%fused_computation.5 | loop fusion | flops 29359616 | bytes 14684160 | tf_op jit(solution)/shard_map/reduce_sum | solution.py:26
  72.3 0.0 copy-start.2
  72.3 0.0 copy-start.3
  72.3 0.0 copy-start.4
  72.3 208.5 %all-gather.3.cloned.1.call-done = bf16[14336,2,384]{2,0,1:T(8,128)(2,1)} async-done(((bf16[1792,2,384]{2,0,1:T(8,128)(2,1)}), bf16[14336,2,384]{2,0,1:T(8,128)(2,1)}) %all-gather.3.cloned.1.call-update) | async-done | bytes 22020112 | tf_op jit(solution)/shard_map/all_gather | solution.py:37
  280.8 26.1 %copy.18 = bf16[14336,2,384]{0,2,1:T(8,128)(2,1)} copy(bf16[14336,2,384]{2,0,1:T(8,128)(2,1)} %all-gather.3.cloned.1.call-done) | data formatting | bytes 44040192 | tf_op jit(solution)/shard_map/all_gather | solution.py:37
  306.9 0.0 copy-done.2
  306.9 0.0 copy-done.3
  306.9 0.0 copy-done.4
  306.9 17.8 %add_convert_fusion.1 = bf16[512,2,384]{2,0,1:T(8,128)(2,1)S(1)} fusion(bf16[14336,2,384]{0,2,1:T(8,128)(2,1)} %copy.18, bf16[512,14336]{1,0:T(8,128)(2,1)} %param.8, f32[14336]{0:T(1024)S(1)} %copy-done.2, f32[14336]{0:T(1024)S(1)} %copy-done.3, f32[512]{0:T(512)S(1)} %add_rsqrt_fusion, f32[512]{0:T(512)S(1)} %broadcast_multiply_fusion, ...), kind=kOutput, calls=%fused_computation.23 | convolution fusion | flops 11319115776 | bytes 37608448 | tf_op jit(solution)/shard_map/dot_general | solution.py:39
  324.7 0.0 copy-start
  324.7 0.9 copy-done
  325.6 0.6 subtract_select_fusion
  326.2 2.0 fusion.30
  328.2 2.3 convolution_convert_fusion.1
  330.5 0.0 all-gather.5.cloned.1.call-update
  330.6 11.5 %reshape.49 = bf16[896,16,256]{2,1,0:T(8,128)(2,1)} reshape(bf16[896,32,128]{2,1,0:T(8,128)(2,1)} %param.13) | data formatting | bytes 14680064 | tf_op jit(solution)/shard_map/reshape | solution.py:63
  342.0 25.0 %all-gather.5.cloned.1.call-done = bf16[512,4096]{0,1:T(8,128)(2,1)} async-done(((bf16[512,256]{0,1:T(8,128)(2,1)}), bf16[512,4096]{0,1:T(8,128)(2,1)}) %all-gather.5.cloned.1.call-update) | async-done | bytes 4194320 | tf_op jit(solution)/shard_map/all_gather | solution.py:59
  367.0 17.4 %convolution_convert_fusion = bf16[16,512,896]{2,1,0:T(8,128)(2,1)} fusion(bf16[512,16,256]{0,2,1:T(8,128)(2,1)} %bitcast.26, bf16[896,16,256]{2,1,0:T(8,128)(2,1)} %reshape.49), kind=kOutput, calls=%fused_computation.17 | convolution fusion | flops 3765436416 | bytes 26214400 | tf_op jit(solution)/shard_map/sgk,dgk->gsd/dot_general | solution.py:64
  384.4 0.0 copy-start.1
  384.4 7.4 %convert_reduce_fusion.1 = f32[512,896]{1,0:T(8,128)S(1)} fusion(bf16[16,512,896]{2,1,0:T(8,128)(2,1)} %convolution_convert_fusion), kind=kLoop, calls=%fused_computation.9 | loop fusion | flops 14221312 | bytes 16515072 | tf_op jit(solution)/shard_map/reduce_sum | solution.py:68
  391.8 0.0 copy-done.1
  391.8 1.0 add_convert_fusion
  (3 shorter events, 0.0 us)
Async XLA Ops:
  6.5 274.3 %all-gather.3.cloned.1.call-start = ((), (), s32[]{:S(2)}) async-start(), calls=%async_computation.1 | async-start | bytes 24772608 | tf_op jit(solution)/shard_map/all_gather | solution.py:37
  52.8 0.7 copy-start.5
  52.9 314.2 %all-gather.5.cloned.1.call-start = ((), (), s32[]{:S(2)}) async-start(), calls=%async_computation.2 | async-start | bytes 4456448 | tf_op jit(solution)/shard_map/all_gather | solution.py:59
  72.3 234.6 %copy-start.2 = (f32[14336]{0:T(1024)S(1)}, f32[14336]{0:T(1024)}, u32[]{:S(2)}) copy-start(f32[14336]{0:T(1024)} %param.10) | copy-start | bytes 172036
  72.3 234.6 %copy-start.3 = (f32[14336]{0:T(1024)S(1)}, f32[14336]{0:T(1024)}, u32[]{:S(2)}) copy-start(f32[14336]{0:T(1024)} %param.9) | copy-start | bytes 172036
  72.3 234.6 %copy-start.4 = (f32[2,384]{1,0:T(2,128)S(1)}, f32[2,384]{1,0:T(2,128)}, u32[]{:S(2)}) copy-start(f32[2,384]{1,0:T(2,128)} %param.12) | copy-start | bytes 9220
  324.7 0.9 copy-start
  384.4 7.4 %copy-start.1 = (f32[896]{0:T(1024)S(1)}, f32[896]{0:T(1024)}, u32[]{:S(2)}) copy-start(f32[896]{0:T(1024)} %param.14) | copy-start | bytes 10756
Sparse Core Ops, SparseCore 0:
  53.0 227.7 all-gather.2
  330.7 36.3 all-gather.4
where the time goes:
time: 401 us; the launch traced here: 400 us
  waiting for transfers between devices  233 us (58%)
  local copies, waits for them, and re-layouts  43.3 us (11%)
  blocking collectives  41.7 us (10%)
  matrix products  40.1 us (10%)
  other arithmetic  27.6 us (7%)
  between operations  13.5 us (3%)
    all_gather x1, waiting for transfers between devices, shards(): weight_piece = lax.all_gather(regrouped, 'rep', axis=0, tiled=True)  208 us
    all_to_all x1, blocking collectives, shards(): lax.all_to_all(qkv_weight, 'tp', split_axis=1, concat_axis=0, tiled=True)  41.7 us
    all_gather x1, local copies, waits for them, and re-layouts, shards(): weight_piece = lax.all_gather(regrouped, 'rep', axis=0, tiled=True)  26.1 us
    all_gather x1, waiting for transfers between devices, shards(): everything = lax.all_gather(context, 'tp', axis=1, tiled=True)  25 us
    dot_general x1, matrix products, shards(): projected = jnp.dot(normed, flat_piece, preferred_element_type=jnp.float32)  17.8 us
    dot_general x1, matrix products, shards(): jnp.einsum('sgk,dgk->gsd', context_blocks, weight_blocks, preferred_eleme...  17.4 us
    reduce_sum x1, other arithmetic, layer_norm(): variance = jnp.mean(centred * centred, axis=-1, keepdims=True)  11.6 us
    reshape x1, local copies, waits for them, and re-layouts, shards(): weight_blocks = out_weight.reshape(out_weight.shape[0], groups, group_width)  11.5 us
  transfers between devices with their start and end apart: 2, of which 2 were waited for; matrix products, arithmetic and copies ran while one was open for 8% of the time, Pallas kernels for 0%

commit v1 on v0

v1 whole, which is shorter than its diff:
```python
import functools
import math

import jax
import jax.numpy as jnp
from jax import lax
from jax.experimental import pallas as pl
from jax.experimental.pallas import tpu as pltpu
from jax.sharding import PartitionSpec as P

N_SLOPES = 112
epsilon = 1e-05
MESH = pl.DeviceIdType.MESH
BF = jnp.bfloat16
F32 = jnp.float32


def slope_values(slope_index):
    power = 1 << N_SLOPES.bit_length() - 1
    index_float = slope_index.astype(jnp.float32)
    leading = jnp.exp2(-8.0 * (index_float + 1.0) / power)
    between = jnp.exp2(-4.0 * (2.0 * (index_float - power) + 1.0) / power)
    return jnp.where(slope_index < power, leading, between)


def my_coords():
    r = lax.axis_index("rep")
    t = lax.axis_index("tp")
    y = r // 2
    x = (r % 2) * 2 + t // 8
    z = (t // 2) % 4
    c = t % 2
    return x, y, z, c


def dev(x, y, z, c):
    return (y * 2 + x // 2, (x % 2) * 8 + z * 2 + c)


ROWS = 64
KB = 3584
WR = 112
HW = 384
W_ORDER = (1, 2, 6, 3, 7, 4, 5)
J_ORDER = (0, 1, 3, 2)


def exchange_kernel(
    wt, hid, gain, shift, bias, out,
    hbuf, nrm, act, wbuf, stg, pst, prx, own,
    hs, wl, zs, zr, xs, xr, ys, yr, as_, ar, ds_, dr, ps, pr,
):
    x, y, z, c = my_coords()
    d_model = gain.shape[1]
    xl = x % 2

    bar = pltpu.get_barrier_semaphore()
    partners = []
    for k in range(1, 8):
        partners.append(dev(x, y, (z + k // 2) % 4, (c + k % 2) % 2))
    for d in range(1, 4):
        partners.append(dev((x + d) % 4, y, z, c))
        partners.append(dev(x, (y + d) % 4, z, c))
    for p in partners:
        pl.semaphore_signal(bar, inc=1, device_id=p, device_id_type=MESH)

    def row_of(p, half, cc):
        return pl.multiple_of(p * 256 + half * 128 + cc * 64, 64)

    half = [(z + p) % 2 for p in range(2)]
    loads = []
    for p in range(2):
        cp = pltpu.make_async_copy(
            hid.at[pl.ds(row_of(p, half[p], c), ROWS), :], hbuf.at[p], hs.at[p])
        cp.start()
        loads.append(cp)

    def slot(xx, k):
        s = ((z + 4 - k // 2) % 4) * 2 + (c + k % 2) % 2
        return pl.multiple_of((xx * 8 + s) * WR, 16)

    tp_own = xl * 8 + z * 2 + c
    tp_oth = (1 - xl) * 8 + z * 2 + c
    wloads = []
    for h in range(2):
        a = pltpu.make_async_copy(
            wt.at[tp_own, h], wbuf.at[h, pl.ds(slot(x, 0), WR), :], wl.at[h, 0])
        b = pltpu.make_async_copy(wt.at[tp_oth, h], stg.at[h, 0], wl.at[h, 1])
        a.start()
        b.start()
        wloads.append((a, b))

    pl.semaphore_wait(bar, len(partners))

    def rcopy(src, dst, ss, rs, to):
        return pltpu.make_async_remote_copy(
            src_ref=src, dst_ref=dst, send_sem=ss, recv_sem=rs, device_id=to, device_id_type=MESH)

    sent = []

    def z_copies(h, k):
        zz, cc = (z + k // 2) % 4, (c + k % 2) % 2
        to = dev(x, y, zz, cc)
        a = rcopy(wt.at[xl * 8 + zz * 2 + cc, h],
                  wbuf.at[h, pl.ds(slot(x, 0), WR), :], zs.at[h, k, 0], zr.at[h, k, 0], to)
        b = rcopy(wt.at[(1 - xl) * 8 + zz * 2 + cc, h],
                  stg.at[h, k], zs.at[h, k, 1], zr.at[h, k, 1], to)
        return a, b

    def x_forward(h, k):
        rows = pl.ds(slot(x, k), WR)
        for d, src in ((1, stg.at[h, k]), (3, stg.at[h, k]), (2, wbuf.at[h, rows, :])):
            cp = rcopy(src, wbuf.at[h, rows, :], xs.at[h, d - 1, k], xr.at[h, d - 1, k],
                       dev((x + d) % 4, y, z, c))
            cp.start()
            sent.append(cp)

    for h in range(2):
        for k in W_ORDER:
            for cp in z_copies(h, k):
                cp.start()
                sent.append(cp)
        for cp in wloads[h]:
            cp.wait()
        x_forward(h, 0)

    step = 512
    nblk = KB // step

    def layer_norm(p):
        def body(rb, carry):
            rows = pl.ds(pl.multiple_of(rb * 16, 16), 16)
            acc = jnp.zeros((16, step), F32)
            for i in range(d_model // step):
                acc = acc + hbuf[p, rows, i * step:(i + 1) * step].astype(F32)
            mean = jnp.sum(acc, axis=1, keepdims=True) / d_model
            acc = jnp.zeros((16, step), F32)
            for i in range(d_model // step):
                dlt = hbuf[p, rows, i * step:(i + 1) * step].astype(F32) - mean
                acc = acc + dlt * dlt
            var = jnp.sum(acc, axis=1, keepdims=True) / d_model
            rstd = lax.rsqrt(var + epsilon)
            for i in range(d_model // step):
                cols = slice(i * step, (i + 1) * step)
                dlt = hbuf[p, rows, cols].astype(F32) - mean
                val = dlt * rstd * gain[:, cols] + shift[:, cols]
                o = (i % nblk) * step
                nrm[p, i // nblk, rows, o:o + step] = val.astype(BF)
            return carry

        lax.fori_loop(0, ROWS // 16, body, 0)

    def act_rows(j, p, hf, cc):
        return act.at[j, pl.ds(row_of(p, hf, cc), ROWS), :]

    def y_copy(p, d):
        return rcopy(nrm.at[p, (y + d) % 4], act_rows(4 - d, p, half[p], c),
                     ys.at[p, d - 1], yr.at[p, 4 - d - 1], dev(x, (y + d) % 4, z, c))

    def z_partner(p):
        return (z + 5 - 2 * ((z + p) % 2)) % 4

    def a_copy(j, p):
        ref = act_rows(j, p, half[p], c)
        return rcopy(ref, ref, as_.at[j, p], ar.at[j, p], dev(x, y, z_partner(p), c))

    def d_copy(j, p, lvl):
        hf = half[p] if lvl == 0 else 1 - half[p]
        ref = act_rows(j, p, hf, c)
        return rcopy(ref, ref, ds_.at[j, p, lvl], dr.at[j, p, lvl], dev(x, y, z, 1 - c))

    def start(cp):
        cp.start()
        sent.append(cp)

    for p in range(2):
        loads[p].wait()
        layer_norm(p)
        for d in (1, 3, 2):
            start(y_copy(p, d))
        rows = pl.ds(row_of(p, half[p], c), ROWS)
        act[0, rows, :] = nrm[p, y]
        start(a_copy(0, p))
        start(d_copy(0, p, 0))

    def recv(dst, rs, like):
        rcopy(dst, dst, ps.at[0, 0], rs, like).wait_recv()

    other = dev(x, y, z, 1 - c)

    def w_arrive(h, k):
        recv(wbuf.at[h, pl.ds(slot(x, k), WR), :], zr.at[h, k, 0], other)
        recv(stg.at[h, k], zr.at[h, k, 1], other)
        x_forward(h, k)

    def y_arrive(j, p):
        recv(act_rows(j, p, half[p], c), yr.at[p, j - 1], other)
        start(a_copy(j, p))
        start(d_copy(j, p, 0))

    def a_arrive(j, p):
        recv(act_rows(j, p, 1 - half[p], c), ar.at[j, p], other)
        start(d_copy(j, p, 1))

    def d_arrive(j):
        for p in range(2):
            for lvl in range(2):
                hf = half[p] if lvl == 0 else 1 - half[p]
                recv(act_rows(j, p, hf, 1 - c), dr.at[j, p, lvl], other)

    def w_ready(h):
        for k in range(8):
            for d in range(1, 4):
                recv(wbuf.at[h, pl.ds(slot((x + 4 - d) % 4, k), WR), :], xr.at[h, d - 1, k], other)

    def tile(h, j):
        def body(i, carry):
            rows = pl.ds(pl.multiple_of(i * 256, 256), 256)
            part = jnp.dot(act[j, rows, :], wbuf[h], preferred_element_type=F32)
            if j == 0:
                own[h, rows, :] = part
            else:
                pst[h, j - 1, rows, :] = part.astype(BF)
            return carry

        lax.fori_loop(0, 2, body, 0)
        if j > 0:
            start(rcopy(pst.at[h, j - 1], prx.at[h, 4 - j - 1], ps.at[h, j - 1], pr.at[h, 4 - j - 1],
                        dev(x, (y + j) % 4, z, c)))

    def finish(h):
        for j in range(1, 4):
            recv(prx.at[h, j - 1], pr.at[h, j - 1], other)
        total = own[h] + bias[h:h + 1, :]
        for j in range(3):
            total = total + prx[h, j].astype(F32)
        out[h] = total.astype(BF)

    for k in W_ORDER:
        w_arrive(0, k)
    y_arrive(1, 0)
    y_arrive(3, 0)
    for k in W_ORDER[:4]:
        w_arrive(1, k)
    y_arrive(1, 1)
    y_arrive(3, 1)
    for k in W_ORDER[4:]:
        w_arrive(1, k)
    for p in range(2):
        a_arrive(0, p)
    y_arrive(2, 0)
    w_ready(0)
    d_arrive(0)
    tile(0, 0)
    y_arrive(2, 1)
    for p in range(2):
        a_arrive(1, p)
        a_arrive(3, p)
    for j in (1, 3):
        d_arrive(j)
        tile(0, j)
    for p in range(2):
        a_arrive(2, p)
    d_arrive(2)
    tile(0, 2)
    w_ready(1)
    for j in (1, 3, 2, 0):
        tile(1, j)
    finish(0)
    finish(1)
    for cp in sent:
        cp.wait_send()


def exchange(wt, hidden, gain, shift, bias):
    d_model = hidden.shape[1]
    dma = pltpu.SemaphoreType.DMA
    anyspec = pl.BlockSpec(memory_space=pl.ANY)
    vm = pl.BlockSpec(memory_space=pltpu.VMEM)
    return pl.pallas_call(
        exchange_kernel,
        out_shape=jax.ShapeDtypeStruct((2, 512, HW), BF),
        in_specs=[anyspec, anyspec, vm, vm, vm],
        out_specs=vm,
        scratch_shapes=[
            pltpu.VMEM((2, ROWS, d_model), BF),
            pltpu.VMEM((2, 4, ROWS, KB), BF),
            pltpu.VMEM((4, 512, KB), BF),
            pltpu.VMEM((2, KB, HW), BF),
            pltpu.VMEM((2, 8, WR, HW), BF),
            pltpu.VMEM((2, 3, 512, HW), BF),
            pltpu.VMEM((2, 3, 512, HW), BF),
            pltpu.VMEM((2, 512, HW), F32),
            dma((2,)), dma((2, 2)),
            dma((2, 8, 2)), dma((2, 8, 2)),
            dma((2, 3, 8)), dma((2, 3, 8)),
            dma((2, 3)), dma((2, 3)),
            dma((4, 2)), dma((4, 2)),
            dma((4, 2, 2)), dma((4, 2, 2)),
            dma((2, 3)), dma((2, 3)),
        ],
        compiler_params=pltpu.CompilerParams(
            collective_id=0, has_side_effects=True, vmem_limit_bytes=60 * 1024 * 1024),
        name="exchange_qkv",
    )(wt, hidden, gain, shift, bias)


def shards(hidden, ln_gain, ln_shift, qkv_weight, qkv_bias, out_weight, out_bias, slope_index):
    seq_rows = hidden.shape[0]
    heads_here = qkv_bias.shape[0]
    head_size = qkv_bias.shape[1] // 3
    wt = jnp.transpose(qkv_weight, (1, 0, 2)).reshape(16, 2, qkv_weight.shape[0], HW)
    qkv = exchange(wt, hidden, ln_gain.reshape(1, -1), ln_shift.reshape(1, -1), qkv_bias)
    query = qkv[:, :, :head_size]
    keys = qkv[:, :, head_size : 2 * head_size]
    values = qkv[:, :, 2 * head_size :]
    slopes = slope_values(slope_index)
    scores = jnp.einsum(
        "hsa,hta->hst", query, keys, preferred_element_type=jnp.float32
    ) / math.sqrt(head_size)
    position = lax.iota(jnp.int32, seq_rows)
    distance = (position[:, None] - position[None, :]).astype(jnp.float32)
    scores = scores - slopes[:, None, None] * distance
    scores = jnp.where(distance >= 0.0, scores, -1e30)
    highest = jnp.max(scores, axis=-1, keepdims=True)
    powered = jnp.exp(scores - highest)
    attention = (powered / jnp.sum(powered, axis=-1, keepdims=True)).astype(jnp.bfloat16)
    context = jnp.einsum(
        "hst,hta->sha", attention, values, preferred_element_type=jnp.float32
    ).astype(jnp.bfloat16)
    context = context.reshape(seq_rows, heads_here * head_size)
    everything = lax.all_gather(context, "tp", axis=1, tiled=True)
    out_matrix = out_weight.reshape(out_weight.shape[0], -1)
    result = jnp.einsum("sk,dk->sd", everything, out_matrix, preferred_element_type=jnp.float32)
    result = result + out_bias
    return result.astype(jnp.bfloat16)


def solution(mesh):
    return jax.shard_map(
        shards,
        mesh=mesh,
        in_specs=(
            P("rep", None),
            P(),
            P(),
            P(("rep", "tp"), None, None),
            P("tp", None),
            P("tp", None, None),
            P("tp"),
            P("tp"),
        ),
        out_specs=P("rep", "tp"),
        check_vma=False,
    )
```

time: 401 us -> 188 us (0.47)
  waiting for transfers between devices: 233 us -> 36.1 us
  Pallas kernels: 0 us -> 114 us
  blocking collectives: 41.7 us -> 0 us
  local copies, waits for them, and re-layouts: 43.3 us -> 4.33 us
  other arithmetic: 27.6 us -> 1.1 us
  matrix products: 40.1 us -> 18.8 us
    all_gather x1 -> x0, waiting for transfers between devices: 208 us -> none  [shards(): weight_piece = lax.all_gather(regrouped, 'rep', axis=0, tiled=True)]
    pallas_call x0 -> x1, Pallas kernels: none -> 114 us  [exchange(): pl.pallas_call(exchange_kernel, out_shape=jax.ShapeDtypeStruct((2, 512, H...]
    all_to_all x1 -> x0, blocking collectives: 41.7 us -> none  [shards(): lax.all_to_all(qkv_weight, 'tp', split_axis=1, concat_axis=0, tiled=True)]
    reduce_sum x3 -> x0, other arithmetic: 26.2 us -> none  [the longest x1 11.6 us: layer_norm(): variance = jnp.mean(centred * centred, axis=-1, keepdims=True)]
    all_gather x1 -> x0, local copies, waits for them, and re-layouts: 26.1 us -> none  [shards(): weight_piece = lax.all_gather(regrouped, 'rep', axis=0, tiled=True)]
    dot_general x4 -> x3, matrix products: 38.1 us -> 16.6 us  [the longest x1 11.1 us: shards(): jnp.einsum('sk,dk->sd', everything, out_matrix, preferred_element_type=jn...]
    reshape x1 -> x0, local copies, waits for them, and re-layouts: 11.5 us -> none  [shards(): weight_blocks = out_weight.reshape(out_weight.shape[0], groups, group_width)]
    all_gather x1, waiting for transfers between devices: 25 us -> 36.1 us  [shards(): everything = lax.all_gather(context, 'tp', axis=1, tiled=True)]
  transfers between devices with their start and end apart: 2 -> 1, of which waited for: 2 -> 1; matrix products, arithmetic and copies ran while one was open for 8% -> 0% of each run, Pallas kernels for 0% -> 0%
where the time goes in v1:
time: 188 us
  Pallas kernels  114 us (61%)
  waiting for transfers between devices  36.1 us (19%)
  matrix products  18.8 us (10%)
  between operations  13.4 us (7%)
  local copies, waits for them, and re-layouts  4.33 us (2%)
    pallas_call x1, Pallas kernels, exchange(): pl.pallas_call(exchange_kernel, out_shape=jax.ShapeDtypeStruct((2, 512, H...  114 us
    all_gather x1, waiting for transfers between devices, shards(): everything = lax.all_gather(context, 'tp', axis=1, tiled=True)  36.1 us
    dot_general x1, matrix products, shards(): jnp.einsum('sk,dk->sd', everything, out_matrix, preferred_element_type=jn...  11.1 us
    transpose x1, local copies, waits for them, and re-layouts, shards(): jnp.transpose(qkv_weight, (1, 0, 2)).reshape(16, 2, qkv_weight.shape[0], HW)  4.32 us
  transfers between devices with their start and end apart: 1, of which 1 were waited for; matrix products, arithmetic and copies ran while one was open for 0% of the time, Pallas kernels for 0%

profile of v1, /device:TPU:1, one launch (start us, length us, event | category | flops | bytes accessed | tf_op | source)
XLA Modules:
  0.0 187.8 jit_solution(18113721734460500966)
XLA Ops:
  6.5 0.0 all-gather.2.cloned.1.call-start
  6.5 0.2 broadcast_compare_fusion
  6.8 0.1 subtract_convert_fusion
  6.9 0.7 compare_select_fusion
  7.6 4.3 %copy.9 = bf16[32,112,384]{2,1,0:T(8,128)(2,1)} copy(bf16[32,112,384]{2,0,1:T(8,128)(2,1)} %bitcast.16) | data formatting | bytes 5505024 | tf_op jit(solution)/shard_map/transpose | solution.py:312
  12.0 114.1 %exchange_qkv.1 = bf16[2,512,384]{2,1,0:T(8,128)(2,1)} custom-call(bf16[16,2,112,384]{3,2,1,0:T(8,128)(2,1)} %bitcast.15, bf16[512,14336]{1,0:T(8,128)(2,1)} %hid.1, f32[1,14336]{1,0:T(1,128)} %bitcast.18, f32[1,14336]{1,0:T(1,128)} %bitcast.19, f32[2,384]{1,0:T(2,128)} %bias.1), custom_call_target="tpu_custom_call" | custom-call | tf_op jit(solution)/shard_map/exchange_qkv/pallas_call | solution.py:280
  126.1 0.0 copy-start
  126.1 2.1 %fusion.16 = f32[2,512]{1,0:T(2,128)S(1)} fusion(f32[512,512]{0,1:T(8,128)S(1)} %subtract_convert_fusion, f32[2]{0:T(128)S(1)} %compare_select_fusion, pred[512,512]{0,1:T(8,128)(4,1)S(1)} %broadcast_compare_fusion, bf16[2,512,384]{2,1,0:T(8,128)(2,1)} %exchange_qkv.1), kind=kOutput, calls=%fused_computation.18 | convolution fusion | flops 137363968 | bytes 1839112 | tf_op jit(solution)/shard_map/sub | solution.py:326
  128.2 0.0 copy-done
  128.2 2.0 %subtract_select_fusion = f32[2,512,512]{1,2,0:T(8,128)} fusion(f32[512,512]{0,1:T(8,128)S(1)} %subtract_convert_fusion, f32[2]{0:T(128)S(1)} %compare_select_fusion, pred[512,512]{0,1:T(8,128)(4,1)S(1)} %broadcast_compare_fusion, bf16[2,512,384]{2,1,0:T(8,128)(2,1)S(1)} %copy-done), kind=kOutput, calls=%fused_computation.6 | convolution fusion | flops 136314880 | bytes 3932672 | tf_op jit(solution)/shard_map/hsa,hta->hst/dot_general | solution.py:318
  130.2 0.0 copy-start.1
  130.2 3.6 %convolution_convert_fusion = bf16[2,128,512]{2,1,0:T(8,128)(2,1)} fusion(f32[2,512]{1,0:T(2,128)S(1)} %fusion.16, bf16[2,512,384]{2,1,0:T(8,128)(2,1)S(1)} %copy-done, f32[2,512,512]{1,2,0:T(8,128)} %subtract_select_fusion), kind=kOutput, calls=%fused_computation.8 | convolution fusion | flops 135923200 | bytes 4722688 | tf_op jit(solution)/shard_map/hst,hta->sha/dot_general | solution.py:328
  133.8 0.0 all-gather.2.cloned.1.call-update
  133.8 36.1 %all-gather.2.cloned.1.call-done = bf16[512,4096]{0,1:T(8,128)(2,1)} async-done(((bf16[512,256]{0,1:T(8,128)(2,1)}), bf16[512,4096]{0,1:T(8,128)(2,1)}) %all-gather.2.cloned.1.call-update) | async-done | bytes 4194320 | tf_op jit(solution)/shard_map/all_gather | solution.py:332
  169.9 0.0 copy-done.1
  169.9 11.1 %add_convert_fusion = bf16[512,896]{1,0:T(8,128)(2,1)} fusion(bf16[512,4096]{0,1:T(8,128)(2,1)} %all-gather.2.cloned.1.call-done, bf16[112,8,32,128]{3,2,1,0:T(8,128)(2,1)} %bitcast.20, f32[896]{0:T(1024)S(1)} %copy-done.1), kind=kOutput, calls=%fused_computation.7 | convolution fusion | flops 3759013888 | bytes 12455424 | tf_op jit(solution)/shard_map/sk,dk->sd/dot_general | solution.py:334
Async XLA Ops:
  6.5 163.4 %all-gather.2.cloned.1.call-start = ((), (), s32[]{:S(2)}) async-start(), calls=%async_computation | async-start | bytes 4456448 | tf_op jit(solution)/shard_map/all_gather | solution.py:332
  126.1 2.1 %copy-start = (bf16[2,512,384]{2,1,0:T(8,128)(2,1)S(1)}, bf16[2,512,384]{2,1,0:T(8,128)(2,1)}, u32[]{:S(2)}) copy-start(bf16[2,512,384]{2,1,0:T(8,128)(2,1)} %exchange_qkv.1) | copy-start | bytes 2359300
  130.2 39.7 %copy-start.1 = (f32[896]{0:T(1024)S(1)}, f32[896]{0:T(1024)}, u32[]{:S(2)}) copy-start(f32[896]{0:T(1024)} %param.14) | copy-start | bytes 10756
Sparse Core Ops, SparseCore 0:
  133.9 35.9 all-gather.1

commit v2 on v0

v2 whole, which is shorter than its diff:
```python
import math

import jax
import jax.numpy as jnp
from jax import lax
from jax.experimental import pallas as pl
from jax.experimental.pallas import tpu as pltpu
from jax.sharding import PartitionSpec as P

N_SLOPES = 112
epsilon = 1e-05
MESH = pl.DeviceIdType.MESH
BF = jnp.bfloat16
F32 = jnp.float32

SEQ = 512
ROWS = 64
KB = 3584
WR = 112
GW = 256
HD = 128
OC = 128
W_ORDER = (1, 2, 6, 3, 7, 4, 5)


def slope_values(slope_index):
    power = 1 << N_SLOPES.bit_length() - 1
    index_float = slope_index.astype(jnp.float32)
    leading = jnp.exp2(-8.0 * (index_float + 1.0) / power)
    between = jnp.exp2(-4.0 * (2.0 * (index_float - power) + 1.0) / power)
    return jnp.where(slope_index < power, leading, between)


def dev(x, y, z, c):
    return (y * 2 + x // 2, (x % 2) * 8 + z * 2 + c)


def kernel(
    wq, hid, gain, shift, bias, ow, obias, slope_index, out,
    wsrc, wtv, hbuf, nrm, act, wbuf, stg, pst, prx, qkvs, owc, owr, cbuf, acc,
    wl, hs, ol, zs, zr, xs, xr, ys, yr, as_, ar, ds_, dr, ps, pr, cs, cr, fs, fr,
):
    r = lax.axis_index("rep")
    t = lax.axis_index("tp")
    y = r // 2
    xl = t // 8
    x = (r % 2) * 2 + xl
    z = (t // 2) % 4
    c = t % 2
    x_in = (x // 2) * 2 + (1 - xl)
    d_model = 4 * KB
    other = dev(x, y, z, 1 - c)

    bar = pltpu.get_barrier_semaphore()
    partners = []
    for k in range(1, 8):
        partners.append(dev(x, y, (z + k // 2) % 4, (c + k % 2) % 2))
    for d in range(1, 4):
        partners.append(dev((x + d) % 4, y, z, c))
        partners.append(dev(x, (y + d) % 4, z, c))
        partners.append(dev(x_in, y, (z + d) % 4, c))
    for p in partners:
        pl.semaphore_signal(bar, inc=1, device_id=p, device_id_type=MESH)

    def half(p):
        return (z + p) % 2

    def row_of(p, hf, cc):
        return pl.multiple_of(p * 256 + hf * 128 + cc * 64, 64)

    wload = pltpu.make_async_copy(wq, wsrc, wl.at[0])
    wload.start()

    def h_load(p, hf, lvl, b):
        return pltpu.make_async_copy(
            hid.at[pl.ds(row_of(p, hf, c), ROWS), pl.ds(b * KB, KB)], hbuf.at[p, b], hs.at[p, lvl, b])

    for p in range(2):
        for b in range(4):
            h_load(p, half(p), 0, b).start()

    def o_load(i):
        return pltpu.make_async_copy(ow.at[pl.ds(i * OC, OC)], owc.at[i % 2], ol.at[i])

    def relay_out(i):
        o_load(i).wait()

        def body(b, carry):
            rows = pl.ds(pl.multiple_of(b * 16, 16), 16)
            dst = pl.ds(pl.multiple_of(i * OC + b * 16, 16), 16)
            turned = jnp.swapaxes(owc[i % 2, rows], 0, 1)
            for h in range(32):
                owr[h % 2, dst, (h // 2) * HD:(h // 2 + 1) * HD] = turned[h]
            return carry

        lax.fori_loop(0, OC // 16, body, 0)
        if i + 2 < 7:
            o_load(i + 2).start()

    def relay_weight(col):
        def body(b, carry):
            rows = pl.ds(pl.multiple_of(b * 16, 16), 16)
            turned = jnp.swapaxes(wsrc[rows, :, col * HD:(col + 1) * HD], 0, 1)
            for h in range(32):
                blk = (h % 2) * 3 + col
                wtv[blk // 2, h // 2, rows, (blk % 2) * HD:(blk % 2 + 1) * HD] = turned[h]
            return carry

        lax.fori_loop(0, WR // 16, body, 0)

    wload.wait()
    relay_weight(0)
    relay_weight(1)
    pl.semaphore_wait(bar, len(partners))

    def rcopy(src, dst, ss, rs, to):
        return pltpu.make_async_remote_copy(
            src_ref=src, dst_ref=dst, send_sem=ss, recv_sem=rs, device_id=to, device_id_type=MESH)

    def recv(dst, rs):
        rcopy(dst, dst, zs.at[0, 0, 0], rs, other).wait_recv()

    def slot(xx, k):
        s = ((z + 4 - k // 2) % 4) * 2 + (c + k % 2) % 2
        return pl.ds(pl.multiple_of((xx * 8 + s) * WR, 16), WR)

    tp_own = xl * 8 + z * 2 + c
    tp_oth = (1 - xl) * 8 + z * 2 + c

    def z_copies(g, k):
        zz, cc = (z + k // 2) % 4, (c + k % 2) % 2
        to = dev(x, y, zz, cc)
        return (
            rcopy(wtv.at[g, xl * 8 + zz * 2 + cc], wbuf.at[g, slot(x, 0), :],
                  zs.at[g, k, 0], zr.at[g, k, 0], to),
            rcopy(wtv.at[g, (1 - xl) * 8 + zz * 2 + cc], stg.at[g, k],
                  zs.at[g, k, 1], zr.at[g, k, 1], to),
        )

    def x_copies(g, k):
        rows = slot(x, k)
        side = wtv.at[g, tp_oth] if k == 0 else stg.at[g, k]
        across = wtv.at[g, tp_own] if k == 0 else wbuf.at[g, rows, :]
        return [
            rcopy(src, wbuf.at[g, rows, :], xs.at[g, d, k], xr.at[g, d, k],
                  dev((x + d) % 4, y, z, c))
            for d, src in ((1, side), (3, side), (2, across))
        ]

    def start(copies):
        for cp in copies:
            cp.start()

    def send_weights(g):
        for k in W_ORDER:
            start(z_copies(g, k))
        start(x_copies(g, 0))
        wbuf[g, slot(x, 0), :] = wtv[g, tp_own]

    def w_arrive(g, k):
        recv(wbuf.at[g, slot(x, k), :], zr.at[g, k, 0])
        recv(stg.at[g, k], zr.at[g, k, 1])
        start(x_copies(g, k))

    def w_ready(g):
        for k in range(8):
            for d in range(1, 4):
                recv(wbuf.at[g, slot((x + 4 - d) % 4, k), :], xr.at[g, d, k])

    step = 512
    nblk = KB // step

    def stats(p, rows):
        total = jnp.zeros((16, step), F32)
        for i in range(4 * nblk):
            o = (i % nblk) * step
            total = total + hbuf[p, i // nblk, rows, o:o + step].astype(F32)
        mean = jnp.sum(total, axis=1, keepdims=True) / d_model
        total = jnp.zeros((16, step), F32)
        for i in range(4 * nblk):
            o = (i % nblk) * step
            centred = hbuf[p, i // nblk, rows, o:o + step].astype(F32) - mean
            total = total + centred * centred
        var = jnp.sum(total, axis=1, keepdims=True) / d_model
        return mean, lax.rsqrt(var + epsilon)

    def act_rows(j, p, hf, cc):
        return act.at[j, pl.ds(row_of(p, hf, cc), ROWS), :]

    def y_copy(p, d):
        return rcopy(nrm.at[p, (y + d) % 4], act_rows(4 - d, p, half(p), c),
                     ys.at[p, d], yr.at[p, 4 - d], dev(x, (y + d) % 4, z, c))

    def a_copy(j, p):
        ref = act_rows(j, p, half(p), c)
        to = dev(x, y, (z + 5 - 2 * half(p)) % 4, c)
        return rcopy(ref, ref, as_.at[j, p], ar.at[j, p], to)

    def d_copy(j, p, lvl):
        hf = half(p) if lvl == 0 else 1 - half(p)
        ref = act_rows(j, p, hf, c)
        return rcopy(ref, ref, ds_.at[j, p, lvl], dr.at[j, p, lvl], other)

    def norm_share(p, carry):
        for b in range(4):
            h_load(p, half(p), 0, b).wait()

        def body(rb, inner):
            rows = pl.ds(pl.multiple_of(rb * 16, 16), 16)
            mean, rstd = stats(p, rows)
            for i in range(4 * nblk):
                o = (i % nblk) * step
                centred = hbuf[p, i // nblk, rows, o:o + step].astype(F32) - mean
                val = centred * rstd * gain[i // nblk, :, o:o + step] + shift[i // nblk, :, o:o + step]
                nrm[p, i // nblk, rows, o:o + step] = val.astype(BF)
            return inner

        lax.fori_loop(0, ROWS // 16, body, 0)
        for b in range(4):
            h_load(p, 1 - half(p), 1, b).start()
        start([y_copy(p, d) for d in (1, 3, 2)])
        act[0, pl.ds(row_of(p, half(p), c), ROWS), :] = nrm[p, y]
        d_copy(0, p, 0).start()
        return carry

    def norm_own(p, carry):
        for b in range(4):
            h_load(p, 1 - half(p), 1, b).wait()

        def body(rb, inner):
            rows = pl.ds(pl.multiple_of(rb * 16, 16), 16)
            mean, rstd = stats(p, rows)
            dst = pl.ds(pl.multiple_of(row_of(p, 1 - half(p), c) + rb * 16, 16), 16)
            for i in range(nblk):
                cols = slice(i * step, (i + 1) * step)
                centred = hbuf[p, y, rows, cols].astype(F32) - mean
                val = centred * rstd * gain[y, :, cols] + shift[y, :, cols]
                act[0, dst, cols] = val.astype(BF)
            return inner

        lax.fori_loop(0, ROWS // 16, body, 0)
        d_copy(0, p, 1).start()
        return carry

    def y_arrive(j, p):
        recv(act_rows(j, p, half(p), c), yr.at[p, j])
        start([a_copy(j, p), d_copy(j, p, 0)])

    def a_arrive(j, p):
        recv(act_rows(j, p, 1 - half(p), c), ar.at[j, p])
        d_copy(j, p, 1).start()

    def d_arrive(j):
        for p in range(2):
            for lvl in range(2):
                hf = half(p) if lvl == 0 else 1 - half(p)
                recv(act_rows(j, p, hf, 1 - c), dr.at[j, p, lvl])

    def p_copy(g, j):
        return rcopy(pst.at[g, j], prx.at[g, 4 - j], ps.at[g, j], pr.at[g, 4 - j],
                     dev(x, (y + j) % 4, z, c))

    def tiles(count, which):
        def body(i, carry):
            g, j = which(i)

            def rows_body(b, inner):
                rows = pl.ds(pl.multiple_of(b * 256, 256), 256)
                part = jnp.dot(act[j, rows, :], wbuf[g], preferred_element_type=F32)
                pst[g, j, rows, :] = part.astype(BF)
                return inner

            lax.fori_loop(0, 2, rows_body, 0)

            @pl.when(j > 0)
            def _():
                p_copy(g, j).start()

            return carry

        lax.fori_loop(0, count, body, 0)

    def finish(g):
        for j in range(1, 4):
            recv(prx.at[g, j], pr.at[g, j])

        def body(b, carry):
            rows = pl.ds(pl.multiple_of(b * 128, 128), 128)
            total = pst[g, 0, rows, :].astype(F32) + bias[g]
            for j in range(1, 4):
                total = total + prx[g, j, rows, :].astype(F32)
            qkvs[g, rows, :] = total.astype(BF)
            return carry

        lax.fori_loop(0, 4, body, 0)

    slopes = slope_values(slope_index[...])

    def attend(h):
        def part(i, rows):
            b = h * 3 + i
            return qkvs[b // 2, rows, (b % 2) * HD:(b % 2 + 1) * HD]

        slope = slopes[h:h + 1, :]
        for i in range(4):
            rows = slice(i * 128, (i + 1) * 128)
            width = (i + 1) * 128
            upto = slice(0, width)
            scores = lax.dot_general(
                part(0, rows), part(1, upto), (((1,), (1,)), ((), ())),
                preferred_element_type=F32) / math.sqrt(HD)
            distance = (i * 128 + lax.broadcasted_iota(jnp.int32, (128, width), 0)
                        - lax.broadcasted_iota(jnp.int32, (128, width), 1)).astype(F32)
            scores = jnp.where(distance >= 0.0, scores - slope * distance, -1e30)
            highest = jnp.max(scores, axis=1, keepdims=True)
            powered = jnp.exp(scores - highest)
            attention = (powered / jnp.sum(powered, axis=1, keepdims=True)).astype(BF)
            context = jnp.dot(attention, part(2, upto), preferred_element_type=F32)
            cbuf[h, t, rows, :] = context.astype(BF)

    def source(q, cc):
        return ((xl + q // 4) % 2) * 8 + ((z + 4 - q % 4) % 4) * 2 + cc

    def c_copy(h, q):
        xx = x if q // 4 == 0 else x_in
        ref = cbuf.at[h, t]
        return rcopy(ref, ref, cs.at[h, q], cr.at[h, q], dev(xx, y, (z + q % 4) % 4, c))

    def f_copy(h, q):
        ref = cbuf.at[h, source(q, c)]
        return rcopy(ref, ref, fs.at[h, q], fr.at[h, q], other)

    def send_context(h):
        start([c_copy(h, q) for q in (1, 3, 4, 5, 7, 2, 6)])
        f_copy(h, 0).start()

    def relay_context(h):
        for q in (1, 3, 4, 5, 7, 2, 6):
            recv(cbuf.at[h, source(q, c)], cr.at[h, q])
            f_copy(h, q).start()

    def context_ready(h):
        for q in range(8):
            recv(cbuf.at[h, source(q, 1 - c)], fr.at[h, q])

    def project(h):
        def body(b, carry):
            rows = pl.ds(pl.multiple_of(b * 256, 256), 256)
            left = jnp.concatenate([cbuf[h, s, rows, :] for s in range(16)], axis=1)
            part = lax.dot_general(left, owr[h], (((1,), (1,)), ((), ())), preferred_element_type=F32)
            if h == 0:
                acc[rows, :] = part
            else:
                out[rows, :] = (acc[rows, :] + part + obias[...]).astype(BF)
            return carry

        lax.fori_loop(0, 2, body, 0)

    send_weights(0)
    lax.fori_loop(0, 2, norm_share, 0)
    relay_weight(2)
    o_load(0).start()
    o_load(1).start()
    for k in W_ORDER:
        w_arrive(0, k)
    lax.fori_loop(0, 2, norm_own, 0)
    y_arrive(1, 0)
    y_arrive(3, 0)
    send_weights(1)
    relay_out(0)
    relay_out(1)
    y_arrive(1, 1)
    y_arrive(3, 1)
    for p in range(2):
        pass
    w_ready(0)
    d_arrive(0)
    tiles(1, lambda i: (0, i))
    for k in W_ORDER[:3]:
        w_arrive(1, k)
    a_arrive(1, 0)
    a_arrive(3, 0)
    for k in W_ORDER[3:]:
        w_arrive(1, k)
    y_arrive(2, 0)
    send_weights(2)
    relay_out(2)
    relay_out(3)
    y_arrive(2, 1)
    a_arrive(1, 1)
    a_arrive(3, 1)
    d_arrive(1)
    d_arrive(3)
    tiles(2, lambda i: (0, 1 + 2 * i))
    w_arrive(2, W_ORDER[0])
    w_ready(1)
    tiles(3, lambda i: (1, (1 + 2 * i) % 5))
    for k in W_ORDER[1:]:
        w_arrive(2, k)
    relay_out(4)
    relay_out(5)
    a_arrive(2, 0)
    a_arrive(2, 1)
    d_arrive(2)
    tiles(2, lambda i: (i, 2))
    w_ready(2)
    tiles(2, lambda i: (2, 1 + 2 * i))
    tiles(2, lambda i: (2, 2 - 2 * i))
    relay_out(6)
    finish(0)
    finish(1)
    attend(0)
    send_context(0)
    finish(2)
    attend(1)
    send_context(1)
    relay_context(0)
    context_ready(0)
    project(0)
    relay_context(1)
    context_ready(1)
    project(1)

    for g in range(3):
        for k in range(8):
            if k:
                for cp in z_copies(g, k):
                    cp.wait_send()
            for cp in x_copies(g, k):
                cp.wait_send()
        for j in range(1, 4):
            p_copy(g, j).wait_send()
    for p in range(2):
        for d in range(1, 4):
            y_copy(p, d).wait_send()
            a_copy(d, p).wait_send()
        for j in range(4):
            for lvl in range(2):
                d_copy(j, p, lvl).wait_send()
    for h in range(2):
        for q in range(8):
            if q:
                c_copy(h, q).wait_send()
            f_copy(h, q).wait_send()


def shards(hidden, ln_gain, ln_shift, qkv_weight, qkv_bias, out_weight, out_bias, slope_index):
    dma = pltpu.SemaphoreType.DMA
    anyspec = pl.BlockSpec(memory_space=pl.ANY)
    vm = pl.BlockSpec(memory_space=pltpu.VMEM)
    return pl.pallas_call(
        kernel,
        out_shape=jax.ShapeDtypeStruct((SEQ, out_weight.shape[0]), BF),
        in_specs=[anyspec, anyspec, vm, vm, vm, anyspec, vm, vm],
        out_specs=vm,
        scratch_shapes=[
            pltpu.VMEM((WR, 32, 384), BF),
            pltpu.VMEM((3, 16, WR, GW), BF),
            pltpu.VMEM((2, 4, ROWS, KB), BF),
            pltpu.VMEM((2, 4, ROWS, KB), BF),
            pltpu.VMEM((4, SEQ, KB), BF),
            pltpu.VMEM((3, KB, GW), BF),
            pltpu.VMEM((3, 8, WR, GW), BF),
            pltpu.VMEM((3, 4, SEQ, GW), BF),
            pltpu.VMEM((3, 4, SEQ, GW), BF),
            pltpu.VMEM((3, SEQ, GW), BF),
            pltpu.VMEM((2, OC, 32, HD), BF),
            pltpu.VMEM((2, 896, 2048), BF),
            pltpu.VMEM((2, 16, SEQ, HD), BF),
            pltpu.VMEM((SEQ, 896), F32),
            dma((1,)), dma((2, 2, 4)), dma((7,)),
            dma((3, 8, 2)), dma((3, 8, 2)),
            dma((3, 4, 8)), dma((3, 4, 8)),
            dma((2, 4)), dma((2, 4)),
            dma((4, 2)), dma((4, 2)),
            dma((4, 2, 2)), dma((4, 2, 2)),
            dma((3, 4)), dma((3, 4)),
            dma((2, 8)), dma((2, 8)),
            dma((2, 8)), dma((2, 8)),
        ],
        compiler_params=pltpu.CompilerParams(
            collective_id=0, has_side_effects=True, vmem_limit_bytes=67043328),
        name="attention_block",
    )(
        qkv_weight,
        hidden,
        ln_gain.reshape(4, 1, KB),
        ln_shift.reshape(4, 1, KB),
        qkv_bias.reshape(3, 1, GW),
        out_weight,
        out_bias.reshape(1, -1),
        slope_index.reshape(2, 1),
    )


def solution(mesh):
    return jax.shard_map(
        shards,
        mesh=mesh,
        in_specs=(
            P("rep", None),
            P(),
            P(),
            P(("rep", "tp"), None, None),
            P("tp", None),
            P("tp", None, None),
            P("tp"),
            P("tp"),
        ),
        out_specs=P("rep", "tp"),
        check_vma=False,
    )
```

time: 401 us -> 146 us (0.36)
  waiting for transfers between devices: 233 us -> 0 us
  Pallas kernels: 0 us -> 140 us
  blocking collectives: 41.7 us -> 0 us
  matrix products: 40.1 us -> 0 us
  local copies, waits for them, and re-layouts: 43.3 us -> 6.04 us
  other arithmetic: 27.6 us -> 0 us
  between operations: 13.5 us -> 0.01 us
    all_gather x2 -> x0, waiting for transfers between devices: 233 us -> none  [the longest x1 208 us: shards(): weight_piece = lax.all_gather(regrouped, 'rep', axis=0, tiled=True)]
    pallas_call x0 -> x1, Pallas kernels: none -> 140 us  [shards(): pl.pallas_call(kernel, out_shape=jax.ShapeDtypeStruct((SEQ, out_weight.sh...]
    all_to_all x1 -> x0, blocking collectives: 41.7 us -> none  [shards(): lax.all_to_all(qkv_weight, 'tp', split_axis=1, concat_axis=0, tiled=True)]
    dot_general x4 -> x0, matrix products: 38.1 us -> none  [the longest x1 17.8 us: shards(): projected = jnp.dot(normed, flat_piece, preferred_element_type=jnp.float32)]
    reduce_sum x3 -> x0, other arithmetic: 26.2 us -> none  [the longest x1 11.6 us: layer_norm(): variance = jnp.mean(centred * centred, axis=-1, keepdims=True)]
    all_gather x1 -> x0, local copies, waits for them, and re-layouts: 26.1 us -> none  [shards(): weight_piece = lax.all_gather(regrouped, 'rep', axis=0, tiled=True)]
    reshape x1 -> x3, local copies, waits for them, and re-layouts: 11.5 us -> 3.87 us  [the longest x1 1.32 us: shards(): slope_index.reshape(2, 1)]
  transfers between devices with their start and end apart: 2 -> 0, of which waited for: 2 -> 0; matrix products, arithmetic and copies ran while one was open for 8% -> 0% of each run, Pallas kernels for 0% -> 0%
where the time goes in v2:
time: 146 us
  Pallas kernels  140 us (96%)
  local copies, waits for them, and re-layouts  6.04 us (4%)
    pallas_call x1, Pallas kernels, shards(): pl.pallas_call(kernel, out_shape=jax.ShapeDtypeStruct((SEQ, out_weight.sh...  140 us

profile of v2, /device:TPU:1, one launch (start us, length us, event | category | flops | bytes accessed | tf_op | source)
XLA Modules:
  0.0 146.0 jit_solution(7640346251205435952)
XLA Ops:
  0.0 1.3 copy.9.slope_index
  1.3 1.3 reshape.17.bias
  2.6 1.3 reshape.18.obias
  3.9 139.9 %attention_block.1 = bf16[512,896]{1,0:T(8,128)(2,1)} custom-call(bf16[112,32,384]{2,1,0:T(8,128)(2,1)} %wq.1, bf16[512,14336]{1,0:T(8,128)(2,1)} %hid.1, f32[4,1,3584]{2,1,0:T(1,128)} %bitcast.3, f32[4,1,3584]{2,1,0:T(1,128)} %bitcast.4, f32[3,1,256]{2,1,0:T(1,128)} %reshape.17.bias, bf16[896,32,128]{2,1,0:T(8,128)(2,1)} %ow.1, f32[1,896]{1,0:T(1,128)} %reshape.18.obias, ...), custom_call_target="tpu_custom_call" | custom-call | tf_op jit(solution)/shard_map/attention_block/pallas_call | solution.py:451
  143.8 2.2 %copy.11 = bf16[512,896]{1,0:T(8,128)(2,1)} copy(bf16[512,896]{1,0:T(8,128)(2,1)} %attention_block.1) | data formatting | bytes 1835008

commit v3 on v2

--- a/solution.py
+++ b/solution.py
@@ -218,7 +218,14 @@
         lax.fori_loop(0, ROWS // 16, body, 0)
         for b in range(4):
             h_load(p, 1 - half(p), 1, b).start()
-        start([y_copy(p, d) for d in (1, 3, 2)])
+        @pl.when(p == 0)
+        def _():
+            y_copy(0, 1).start()
+
+        @pl.when(p == 1)
+        def _():
+            start([y_copy(1, 3), y_copy(1, 1), y_copy(0, 3), y_copy(0, 2), y_copy(1, 2)])
+
         act[0, pl.ds(row_of(p, half(p), c), ROWS), :] = nrm[p, y]
         d_copy(0, p, 0).start()
         return carry
@@ -256,53 +263,52 @@
                 hf = half(p) if lvl == 0 else 1 - half(p)
                 recv(act_rows(j, p, hf, 1 - c), dr.at[j, p, lvl])
 
-    def p_copy(g, j):
-        return rcopy(pst.at[g, j], prx.at[g, 4 - j], ps.at[g, j], pr.at[g, 4 - j],
+    def p_copy(g, j, b):
+        rows = pl.ds(pl.multiple_of(b * 256, 256), 256)
+        return rcopy(pst.at[g, j, rows, :], prx.at[g, 4 - j, rows, :], ps.at[g, j, b], pr.at[g, 4 - j, b],
                      dev(x, (y + j) % 4, z, c))
 
     def tiles(count, which):
         def body(i, carry):
-            g, j = which(i)
-
-            def rows_body(b, inner):
-                rows = pl.ds(pl.multiple_of(b * 256, 256), 256)
-                part = jnp.dot(act[j, rows, :], wbuf[g], preferred_element_type=F32)
-                pst[g, j, rows, :] = part.astype(BF)
-                return inner
-
-            lax.fori_loop(0, 2, rows_body, 0)
+            g, j, b = which(i)
+            rows = pl.ds(pl.multiple_of(b * 256, 256), 256)
+            part = jnp.dot(act[j, rows, :], wbuf[g], preferred_element_type=F32)
+            pst[g, j, rows, :] = part.astype(BF)
 
             @pl.when(j > 0)
             def _():
-                p_copy(g, j).start()
+                p_copy(g, j, b).start()
 
             return carry
 
         lax.fori_loop(0, count, body, 0)
 
-    def finish(g):
+    def group_bias(g):
+        parts = [bias[b // 3:b // 3 + 1, (b % 3) * HD:(b % 3 + 1) * HD] for b in (2 * g, 2 * g + 1)]
+        return jnp.concatenate(parts, axis=1)
+
+    def finish(g, b):
+        rows = pl.ds(b * 256, 256)
         for j in range(1, 4):
-            recv(prx.at[g, j], pr.at[g, j])
-
-        def body(b, carry):
-            rows = pl.ds(pl.multiple_of(b * 128, 128), 128)
-            total = pst[g, 0, rows, :].astype(F32) + bias[g]
+            recv(prx.at[g, j, rows, :], pr.at[g, j, b])
+
+        def body(i, carry):
+            part = pl.ds(pl.multiple_of(b * 256 + i * 128, 128), 128)
+            total = pst[g, 0, part, :].astype(F32) + group_bias(g)
             for j in range(1, 4):
-                total = total + prx[g, j, rows, :].astype(F32)
-            qkvs[g, rows, :] = total.astype(BF)
+                total = total + prx[g, j, part, :].astype(F32)
+            qkvs[g, part, :] = total.astype(BF)
             return carry
 
-        lax.fori_loop(0, 4, body, 0)
-
-    slopes = slope_values(slope_index[...])
-
-    def attend(h):
+        lax.fori_loop(0, 2, body, 0)
+
+    def attend(h, b):
         def part(i, rows):
-            b = h * 3 + i
-            return qkvs[b // 2, rows, (b % 2) * HD:(b % 2 + 1) * HD]
-
-        slope = slopes[h:h + 1, :]
-        for i in range(4):
+            n = h * 3 + i
+            return qkvs[n // 2, rows, (n % 2) * HD:(n % 2 + 1) * HD]
+
+        slope = slope_values(jnp.full((1, 1), slope_index[h], jnp.int32))
+        for i in (2 * b, 2 * b + 1):
             rows = slice(i * 128, (i + 1) * 128)
             width = (i + 1) * 128
             upto = slice(0, width)
@@ -321,105 +327,101 @@
     def source(q, cc):
         return ((xl + q // 4) % 2) * 8 + ((z + 4 - q % 4) % 4) * 2 + cc
 
-    def c_copy(h, q):
+    def c_copy(h, b, q):
         xx = x if q // 4 == 0 else x_in
-        ref = cbuf.at[h, t]
-        return rcopy(ref, ref, cs.at[h, q], cr.at[h, q], dev(xx, y, (z + q % 4) % 4, c))
-
-    def f_copy(h, q):
-        ref = cbuf.at[h, source(q, c)]
-        return rcopy(ref, ref, fs.at[h, q], fr.at[h, q], other)
-
-    def send_context(h):
-        start([c_copy(h, q) for q in (1, 3, 4, 5, 7, 2, 6)])
-        f_copy(h, 0).start()
-
-    def relay_context(h):
-        for q in (1, 3, 4, 5, 7, 2, 6):
-            recv(cbuf.at[h, source(q, c)], cr.at[h, q])
-            f_copy(h, q).start()
-
-    def context_ready(h):
+        ref = cbuf.at[h, t, pl.ds(b * 256, 256), :]
+        return rcopy(ref, ref, cs.at[h, b, q], cr.at[h, b, q], dev(xx, y, (z + q % 4) % 4, c))
+
+    def f_copy(h, b, q):
+        ref = cbuf.at[h, source(q, c), pl.ds(b * 256, 256), :]
+        return rcopy(ref, ref, fs.at[h, b, q], fr.at[h, b, q], other)
+
+    C_ORDER = (1, 3, 4, 5, 7, 2, 6)
+
+    def send_context(h, b):
+        start([c_copy(h, b, q) for q in C_ORDER])
+        f_copy(h, b, 0).start()
+
+    def relay_context(h, b):
+        for q in C_ORDER:
+            recv(cbuf.at[h, source(q, c), pl.ds(b * 256, 256), :], cr.at[h, b, q])
+            f_copy(h, b, q).start()
+
+    def context_ready(h, b):
         for q in range(8):
-            recv(cbuf.at[h, source(q, 1 - c)], fr.at[h, q])
-
-    def project(h):
-        def body(b, carry):
-            rows = pl.ds(pl.multiple_of(b * 256, 256), 256)
-            left = jnp.concatenate([cbuf[h, s, rows, :] for s in range(16)], axis=1)
-            part = lax.dot_general(left, owr[h], (((1,), (1,)), ((), ())), preferred_element_type=F32)
-            if h == 0:
-                acc[rows, :] = part
-            else:
-                out[rows, :] = (acc[rows, :] + part + obias[...]).astype(BF)
-            return carry
-
-        lax.fori_loop(0, 2, body, 0)
+            recv(cbuf.at[h, source(q, 1 - c), pl.ds(b * 256, 256), :], fr.at[h, b, q])
+
+    def project(h, b):
+        rows = pl.ds(b * 256, 256)
+        left = jnp.concatenate([cbuf[h, s, rows, :] for s in range(16)], axis=1)
+        part = lax.dot_general(left, owr[h], (((1,), (1,)), ((), ())), preferred_element_type=F32)
+        if h == 0:
+            acc[rows, :] = part
+        else:
+            out[rows, :] = (acc[rows, :] + part + obias[...].reshape(1, 896)).astype(BF)
 
     send_weights(0)
+    relay_weight(2)
+    send_weights(1)
     lax.fori_loop(0, 2, norm_share, 0)
-    relay_weight(2)
     o_load(0).start()
     o_load(1).start()
     for k in W_ORDER:
         w_arrive(0, k)
     lax.fori_loop(0, 2, norm_own, 0)
-    y_arrive(1, 0)
+    y_arrive(1, 1)
     y_arrive(3, 0)
-    send_weights(1)
     relay_out(0)
     relay_out(1)
-    y_arrive(1, 1)
+    for k in W_ORDER:
+        w_arrive(1, k)
+    y_arrive(1, 0)
     y_arrive(3, 1)
-    for p in range(2):
-        pass
+    send_weights(2)
+    for i in range(2, 7):
+        relay_out(i)
     w_ready(0)
     d_arrive(0)
-    tiles(1, lambda i: (0, i))
-    for k in W_ORDER[:3]:
-        w_arrive(1, k)
+    tiles(2, lambda i: (0, 0, i))
     a_arrive(1, 0)
+    a_arrive(3, 1)
+    y_arrive(2, 0)
+    a_arrive(1, 1)
     a_arrive(3, 0)
-    for k in W_ORDER[3:]:
-        w_arrive(1, k)
-    y_arrive(2, 0)
-    send_weights(2)
-    relay_out(2)
-    relay_out(3)
-    y_arrive(2, 1)
-    a_arrive(1, 1)
-    a_arrive(3, 1)
     d_arrive(1)
     d_arrive(3)
-    tiles(2, lambda i: (0, 1 + 2 * i))
-    w_arrive(2, W_ORDER[0])
+    tiles(4, lambda i: (0, 1 + 2 * (i // 2), i % 2))
+    y_arrive(2, 1)
+    for k in W_ORDER:
+        w_arrive(2, k)
     w_ready(1)
-    tiles(3, lambda i: (1, (1 + 2 * i) % 5))
-    for k in W_ORDER[1:]:
-        w_arrive(2, k)
-    relay_out(4)
-    relay_out(5)
+    tiles(6, lambda i: (1, (1 + 2 * (i // 2)) % 5, i % 2))
     a_arrive(2, 0)
     a_arrive(2, 1)
     d_arrive(2)
-    tiles(2, lambda i: (i, 2))
+    tiles(4, lambda i: (i // 2, 2, i % 2))
     w_ready(2)
-    tiles(2, lambda i: (2, 1 + 2 * i))
-    tiles(2, lambda i: (2, 2 - 2 * i))
-    relay_out(6)
-    finish(0)
-    finish(1)
-    attend(0)
-    send_context(0)
-    finish(2)
-    attend(1)
-    send_context(1)
-    relay_context(0)
-    context_ready(0)
-    project(0)
-    relay_context(1)
-    context_ready(1)
-    project(1)
+    tiles(8, lambda i: (2, (1 + 2 * (i % 4) + (i % 4) // 2) % 4, i // 4))
+    for b in range(2):
+        finish(0, b)
+        finish(1, b)
+        attend(0, b)
+        send_context(0, b)
+    finish(2, 0)
+    attend(1, 0)
+    send_context(1, 0)
+    for b in range(2):
+        relay_context(0, b)
+    finish(2, 1)
+    attend(1, 1)
+    send_context(1, 1)
+    for b in range(2):
+        context_ready(0, b)
+        project(0, b)
+    for b in range(2):
+        relay_context(1, b)
+        context_ready(1, b)
+        project(1, b)
 
     for g in range(3):
         for k in range(8):
@@ -429,7 +431,8 @@
             for cp in x_copies(g, k):
                 cp.wait_send()
         for j in range(1, 4):
-            p_copy(g, j).wait_send()
+            for b in range(2):
+                p_copy(g, j, b).wait_send()
     for p in range(2):
         for d in range(1, 4):
             y_copy(p, d).wait_send()
@@ -438,10 +441,11 @@
             for lvl in range(2):
                 d_copy(j, p, lvl).wait_send()
     for h in range(2):
-        for q in range(8):
-            if q:
-                c_copy(h, q).wait_send()
-            f_copy(h, q).wait_send()
+        for b in range(2):
+            for q in range(8):
+                if q:
+                    c_copy(h, b, q).wait_send()
+                f_copy(h, b, q).wait_send()
 
 
 def shards(hidden, ln_gain, ln_shift, qkv_weight, qkv_bias, out_weight, out_bias, slope_index):
@@ -451,7 +455,7 @@
     return pl.pallas_call(
         kernel,
         out_shape=jax.ShapeDtypeStruct((SEQ, out_weight.shape[0]), BF),
-        in_specs=[anyspec, anyspec, vm, vm, vm, anyspec, vm, vm],
+        in_specs=[anyspec, anyspec, vm, vm, vm, anyspec, vm, pl.BlockSpec(memory_space=pltpu.SMEM)],
         out_specs=vm,
         scratch_shapes=[
             pltpu.VMEM((WR, 32, 384), BF),
@@ -474,9 +478,9 @@
             dma((2, 4)), dma((2, 4)),
             dma((4, 2)), dma((4, 2)),
             dma((4, 2, 2)), dma((4, 2, 2)),
-            dma((3, 4)), dma((3, 4)),
-            dma((2, 8)), dma((2, 8)),
-            dma((2, 8)), dma((2, 8)),
+            dma((3, 4, 2)), dma((3, 4, 2)),
+            dma((2, 2, 8)), dma((2, 2, 8)),
+            dma((2, 2, 8)), dma((2, 2, 8)),
         ],
         compiler_params=pltpu.CompilerParams(
             collective_id=0, has_side_effects=True, vmem_limit_bytes=67043328),
@@ -486,10 +490,10 @@
         hidden,
         ln_gain.reshape(4, 1, KB),
         ln_shift.reshape(4, 1, KB),
-        qkv_bias.reshape(3, 1, GW),
+        qkv_bias,
         out_weight,
-        out_bias.reshape(1, -1),
-        slope_index.reshape(2, 1),
+        out_bias,
+        slope_index,
     )
 
 

time: 146 us -> 126 us (0.86)
  Pallas kernels: 140 us -> 124 us
  local copies, waits for them, and re-layouts: 6.04 us -> 2.18 us
    pallas_call x1, Pallas kernels: 140 us -> 124 us  [shards(): pl.pallas_call(kernel, out_shape=jax.ShapeDtypeStruct((SEQ, out_weight.sh...]
    reshape x3 -> x0, local copies, waits for them, and re-layouts: 3.87 us -> none  [the longest x1 1.32 us: shards(): slope_index.reshape(2, 1)]
where the time goes in v3:
time: 126 us
  Pallas kernels  124 us (98%)
  local copies, waits for them, and re-layouts  2.18 us (2%)
    pallas_call x1, Pallas kernels, shards(): pl.pallas_call(kernel, out_shape=jax.ShapeDtypeStruct((SEQ, out_weight.sh...  124 us

profile of v3, /device:TPU:1, one launch (start us, length us, event | category | flops | bytes accessed | tf_op | source)
XLA Modules:
  0.0 125.7 jit_solution(1180549578612463430)
XLA Ops:
  0.0 123.5 %attention_block.1 = bf16[512,896]{1,0:T(8,128)(2,1)} custom-call(bf16[112,32,384]{2,1,0:T(8,128)(2,1)} %wq.1, bf16[512,14336]{1,0:T(8,128)(2,1)} %hid.1, f32[4,1,3584]{2,1,0:T(1,128)} %bitcast.2, f32[4,1,3584]{2,1,0:T(1,128)} %bitcast.3, f32[2,384]{1,0:T(2,128)} %bias.1, bf16[896,32,128]{2,1,0:T(8,128)(2,1)} %ow.1, f32[896]{0:T(1024)} %obias.1, s32[2]{0:T(128)} %slope_index.1), custom_call_target="tpu_custom_call" | custom-call | tf_op jit(solution)/shard_map/attention_block/pallas_call | solution.py:455
  123.5 2.2 %copy.10 = bf16[512,896]{1,0:T(8,128)(2,1)} copy(bf16[512,896]{1,0:T(8,128)(2,1)} %attention_block.1) | data formatting | bytes 1835008
